TPU v7x, 32 devices: a whole 2x2x4 slice. The times are simulated.
32 devices in a mesh: groups: 2 (over y), seq: 4 (over z), head: 2 (over x), rep: 2 (over core).
Axes of the slice: x: 2, y: 2, z: 4, core: 2. Of those that a mesh axis runs over, the one named last changes fastest.
Arguments:
- tokens: bfloat16 [8, 4096], P('groups', ('seq', 'rep')), parts along dimension 0, may hold values from -6 to 6
- attn_gain: float32 [4096], P(('seq', 'rep')), may hold values from 0.25 to 1.75
- ffn_gain: float32 [4096], P(('seq', 'rep')), may hold values from 0.25 to 1.75
- w_query: bfloat16 [4096, 4096], P(('seq', 'rep'), 'head'), may hold values from -0.0625 to 0.0625
- w_key: bfloat16 [4096, 1024], P(('seq', 'rep'), 'head'), may hold values from -0.09375 to 0.09375
- w_value: bfloat16 [4096, 1024], P(('seq', 'rep'), 'head'), may hold values from -0.25 to 0.25
- w_out: bfloat16 [4096, 4096], P('head', ('seq', 'rep')), may hold values from -0.09375 to 0.09375
- w_gate: bfloat16 [4096, 7168], P(('seq', 'rep'), 'head'), may hold values from -0.09375 to 0.09375
- w_up: bfloat16 [4096, 7168], P(('seq', 'rep'), 'head'), may hold values from -0.09375 to 0.09375
- w_down: bfloat16 [7168, 4096], P('head', ('seq', 'rep')), may hold values from -0.0625 to 0.0625
- kv_pool: bfloat16 [2, 8, 4, 128, 1024], P(None, ('groups', 'seq'), 'head', 'rep'), parts along dimension 1, may hold values from -15 to 15
- lengths: int32 [8], P('groups'), parts along dimension 0, may hold values from 1 to 512, 1024 in all
- pool_row: int32 [8], P('groups'), parts along dimension 0, may hold values from 0 to 3, each once
- block_table: int32 [8, 4], P('groups'), parts along dimension 0, may hold values from 0 to 3, each once within a row
Outputs:
- layer_out: bfloat16 [8, 4096], P('groups', ('seq', 'rep')), parts along dimension 0
- kv_decode: bfloat16 [2, 8, 512, 1024], P(None, 'groups', ('seq', 'rep'), 'head'), parts along dimension 1
There are 2 independent parts, one for each index of `groups`. A program takes and returns all parts, laid end to end along the dimension named above; an argument that names none is the same for every part. Nothing has to cross between parts.
Inputs may be any that keep to these rules, and one draw needn't show every extreme that they name: One sequence reaches 512; the lengths sum to 1024. `pool_row`: a permutation of the pool rows. `block_table`: every row is a permutation of the 4 slots.
All inputs are finite; a program needn't handle non-finite values.
Results may differ from a plain program's by a relative error of at most 0.008.
Values may be sent and summed in bfloat16 or wider, within the bound.
A program may use at most 64 MiB of HBM per device.

v0:
```python
import math

import jax
import jax.numpy as jnp
from jax import lax
from jax.sharding import PartitionSpec as P

D = 4096
H = 32
KVH = 8
HD = 128
BLK = 128


EPSILON = 1e-05
ROPE_LOG = math.log(500000.0)
FLOOR_SCORE = -1e30


def combined_all(value, axis, combine):
    everything = jax.tree.map(lambda part: lax.all_gather(part, axis), value)
    leading = jax.tree.map(lambda part: part[0], everything)

    def hop(k, so_far):
        return combine(so_far, jax.tree.map(lambda part: part[k], everything))

    return lax.fori_loop(1, lax.axis_size(axis), hop, leading)


def rotate(values, positions):
    half_dim = values.shape[-1] // 2
    freq_table = jnp.exp(
        jnp.arange(half_dim, dtype=jnp.float32) * (-2.0 * ROPE_LOG / values.shape[-1])
    )
    angles = positions[:, None, None] * freq_table
    cosine = jnp.cos(angles)
    sine_part = jnp.sin(angles)
    first_half = values[..., :half_dim]
    second_half = values[..., half_dim:]
    return jnp.concatenate(
        [
            first_half * cosine - second_half * sine_part,
            second_half * cosine + first_half * sine_part,
        ],
        axis=-1,
    )


def combine(first, second):
    top_a, mass_a, summed_a = first
    top_b, mass_b, summed_b = second
    largest = jnp.maximum(top_a, top_b)
    scale_a = jnp.exp(top_a - largest)
    scale_b = jnp.exp(top_b - largest)
    return (
        largest,
        mass_a * scale_a + mass_b * scale_b,
        summed_a * scale_a[..., None] + summed_b * scale_b[..., None],
    )


def partial_attention(queries, key_rows, value_rows, usable):
    factor = 1.0 / math.sqrt(queries.shape[-1])
    scores = (
        jnp.einsum("sngd,stnd->sngt", queries, key_rows, preferred_element_type=jnp.float32)
        * factor
    )
    scores = jnp.where(usable[:, None, None, :], scores, FLOOR_SCORE)
    highest = jnp.max(scores, axis=-1)
    weights = jnp.where(usable[:, None, None, :], jnp.exp(scores - highest[..., None]), 0.0)
    totals = jnp.sum(weights, axis=-1)
    summed = jnp.einsum(
        "sngt,stnd->sngd",
        weights.astype(jnp.bfloat16),
        value_rows,
        preferred_element_type=jnp.float32,
    )
    return (highest, totals, summed)


def finish(merged, queries, key_own, value_own):
    highest, totals, summed = merged
    factor = 1.0 / math.sqrt(queries.shape[-1])
    own_score = (
        jnp.sum(queries.astype(jnp.float32) * key_own.astype(jnp.float32)[:, :, None, :], axis=-1)
        * factor
    )
    largest = jnp.maximum(highest, own_score)
    kept_scale = jnp.exp(highest - largest)
    new_scale = jnp.exp(own_score - largest)
    denominator = totals * kept_scale + new_scale
    mixed = (
        summed * kept_scale[..., None]
        + new_scale[..., None] * value_own.astype(jnp.float32)[:, :, None, :]
    )
    return mixed / denominator[..., None]


def shards(
    tokens,
    attn_gain,
    ffn_gain,
    w_query,
    w_key,
    w_value,
    w_out,
    w_gate,
    w_up,
    w_down,
    kv_pool,
    lengths,
    pool_row,
    block_table,
):
    seq_count = tokens.shape[0]
    per_group = H // KVH
    kv_local = w_key.shape[1] // HD
    residual = tokens.astype(jnp.float32)
    square_sum = lax.psum(jnp.sum(residual * residual, axis=1), ("seq", "rep"))
    normed = (residual * lax.rsqrt(square_sum / D + EPSILON)[:, None] * attn_gain).astype(
        jnp.bfloat16
    )
    queries, keys_new, values_new = lax.psum(
        (
            jnp.dot(normed, w_query, preferred_element_type=jnp.float32),
            jnp.dot(normed, w_key, preferred_element_type=jnp.float32),
            jnp.dot(normed, w_value, preferred_element_type=jnp.float32),
        ),
        ("seq", "rep"),
    )
    positions = lengths.astype(jnp.float32)
    rot_queries = rotate(queries.reshape(seq_count, -1, HD), positions).astype(jnp.bfloat16)
    rot_keys = rotate(keys_new.reshape(seq_count, kv_local, HD), positions).astype(jnp.bfloat16)
    new_values = values_new.reshape(seq_count, kv_local, HD).astype(jnp.bfloat16)
    slot_count = kv_pool.shape[2]
    half_rows = kv_pool.shape[3]
    feat_width = kv_pool.shape[4]
    head_count = lax.axis_size("head")
    seq_devices = lax.axis_size("seq")
    row_here = lax.axis_index("seq")
    head_here = lax.axis_index("head")
    rep_here = lax.axis_index("rep")
    seq_ids = jnp.arange(seq_count, dtype=jnp.int32)
    owner_seq = jnp.sum(jnp.where(pool_row == row_here, seq_ids, 0))
    table_row = lax.dynamic_index_in_dim(block_table, owner_seq, 0, keepdims=False)
    length_here = lax.dynamic_index_in_dim(lengths, owner_seq, 0, keepdims=False)
    block_count = table_row.shape[0]
    slot_ids = head_here * slot_count + jnp.arange(slot_count, dtype=jnp.int32)
    block_ids = jnp.arange(block_count, dtype=jnp.int32)
    block_of_slot = jnp.sum(
        jnp.where(table_row[None, :] == slot_ids[:, None], block_ids[None, :], 0), axis=1
    )
    token_pos = (
        block_of_slot[:, None] * BLK
        + rep_here * half_rows
        + jnp.arange(half_rows, dtype=jnp.int32)[None, :]
    )
    is_live = token_pos < length_here
    pool_local = kv_pool[:, 0]
    cleaned = jnp.where(is_live[None, :, :, None], pool_local, jnp.zeros((), jnp.bfloat16))
    local_slot = table_row - head_here * slot_count
    is_held = (local_slot >= 0) & (local_slot < slot_count)
    picked = jnp.take(cleaned, jnp.clip(local_slot, 0, slot_count - 1), axis=1)
    picked = jnp.where(is_held[None, :, None, None], picked, jnp.zeros((), jnp.bfloat16))
    parted = picked.reshape(2, block_count, half_rows, head_count, feat_width // head_count)
    parted = jnp.transpose(parted, (0, 1, 3, 2, 4)).reshape(
        2, 1, block_count * head_count, half_rows, feat_width // head_count
    )
    arrived = lax.all_to_all(parted, ("seq", "head"), split_axis=2, concat_axis=1, tiled=True)
    by_row = jnp.sum(
        arrived.reshape(2, seq_devices, head_count, half_rows, feat_width // head_count), axis=2
    )
    decoded = jnp.take(by_row, pool_row, axis=1)
    first_pos = lax.axis_index(("seq", "rep")) * half_rows
    usable = first_pos + jnp.arange(half_rows, dtype=jnp.int32)[None, :] < lengths[:, None]
    key_rows = decoded[0].reshape(seq_count, half_rows, kv_local, HD)
    value_rows = decoded[1].reshape(seq_count, half_rows, kv_local, HD)
    query_groups = rot_queries.reshape(seq_count, kv_local, per_group, HD)
    merged = combined_all(
        partial_attention(query_groups, key_rows, value_rows, usable), ("seq", "rep"), combine
    )
    mixed = finish(merged, query_groups, rot_keys, new_values)
    attn_heads = mixed.reshape(seq_count, -1).astype(jnp.bfloat16)
    attn_proj = lax.psum(jnp.dot(attn_heads, w_out, preferred_element_type=jnp.float32), "head")
    middle = residual + attn_proj
    square_mid = lax.psum(jnp.sum(middle * middle, axis=1), ("seq", "rep"))
    normed_mid = (middle * lax.rsqrt(square_mid / D + EPSILON)[:, None] * ffn_gain).astype(
        jnp.bfloat16
    )
    gate_sum, up_sum = lax.psum(
        (
            jnp.dot(normed_mid, w_gate, preferred_element_type=jnp.float32),
            jnp.dot(normed_mid, w_up, preferred_element_type=jnp.float32),
        ),
        ("seq", "rep"),
    )
    hidden = (jax.nn.silu(gate_sum) * up_sum).astype(jnp.bfloat16)
    down_part = lax.psum(jnp.dot(hidden, w_down, preferred_element_type=jnp.float32), "head")
    return ((middle + down_part).astype(jnp.bfloat16), decoded)


def solution(mesh):
    in_specs = (
        P("groups", ("seq", "rep")),
        P(("seq", "rep")),
        P(("seq", "rep")),
        P(("seq", "rep"), "head"),
        P(("seq", "rep"), "head"),
        P(("seq", "rep"), "head"),
        P("head", ("seq", "rep")),
        P(("seq", "rep"), "head"),
        P(("seq", "rep"), "head"),
        P("head", ("seq", "rep")),
        P(None, ("groups", "seq"), "head", "rep", None),
        P("groups"),
        P("groups"),
        P("groups", None),
    )
    out_specs = (P("groups", ("seq", "rep")), P(None, "groups", ("seq", "rep"), "head"))
    return jax.shard_map(shards, mesh=mesh, in_specs=in_specs, out_specs=out_specs, check_vma=False)
```

profile of v0, /device:TPU:0, one launch (start us, length us, event | category | flops | bytes accessed | tf_op | source)
XLA Modules:
  0.0 228.1 jit_solution(14195737059538864200)
XLA Ops:
  7.2 0.0 copy-start
  7.2 1.4 compare_select_fusion.2
  10.6 0.7 compare_and_fusion.1
  11.3 0.7 fusion.27
  12.0 0.2 fusion.25
  12.2 1.2 dynamic_slice.39
  13.4 0.7 add_compare_fusion
  14.1 1.1 bitcast_select_fusion
  15.3 1.6 gather_fusion
  16.9 1.8 reshape.262
  18.7 0.0 copy-start.6
  18.8 0.0 copy-start.2
  18.8 0.0 copy-start.3
  18.8 1.1 fusion.4
  19.9 0.0 copy-start.5
  19.9 1.2 copy.45
  21.1 7.3 %all-to-all-start = ((bf16[2,1,8,64,512]{4,3,0,1,2:T(8,128)(2,1)}), bf16[2,1,8,64,512]{4,3,0,1,2:T(8,128)(2,1)S(1)}, u32[]{:S(2)}, u32[]{:S(2)}) async-start(bf16[2,1,8,64,512]{4,3,0,1,2:T(8,128)(2,1)} %bitcast.69), calls=%async_computation | async-start | bytes 2097152 | tf_op jit(solution)/shard_map/all_to_all | solution.py:169
  28.4 0.0 all-reduce.4.cloned.1.call-start
  28.4 0.1 fusion.22
  28.5 28.3 %psum.63 = f32[4]{0:T(128)S(1)} all-reduce(f32[4]{0:T(128)S(1)} %fusion.22), channel_id=1, replica_groups=mesh['groups'=2,'seq'=4,'head'=2,'rep'=2] {'seq','rep'}, use_global_device_ids=true, to_apply=%region_1.0 | all-reduce | flops 4 | bytes 32 | tf_op jit(solution)/shard_map/psum | solution.py:119
  56.9 1.2 fusion.33
  58.1 1.3 fusion.31
  59.4 0.4 convolution_bitcast_fusion
  59.9 28.2 %all-reduce.1 = (f32[4,16,128]{2,1,0:T(8,128)S(1)}, f32[4,4,128]{2,1,0:T(4,128)S(1)}, bf16[4,512]{1,0:T(4,128)(2,1)S(1)}) all-reduce(f32[4,16,128]{2,1,0:T(8,128)S(1)} %bitcast.73, f32[4,4,128]{2,1,0:T(4,128)S(1)} %reshape.234, f32[4,512]{1,0:T(4,128)S(1)} %fusion.31), channel_id=1, replica_groups=mesh['groups'=2,'seq'=4,'head'=2,'rep'=2] {'seq','rep'}, use_global_device_ids=true, to_apply=%region_2.0 | all-reduce | flops 12288 | bytes 94208 | tf_op jit(solution)/shard_map/psum | solution.py:123
  88.1 0.1 multiply_cosine_fusion
  88.2 0.1 subtract_convert_fusion.1
  88.3 0.1 maximum_convert_fusion
  88.3 0.1 subtract_convert_fusion
  88.4 0.2 multiply_reduce_fusion
  88.6 0.1 broadcast_compare_fusion
  88.7 1.1 reduce_sum.69
  89.8 1.1 copy.40
  90.9 0.6 gather_fusion.1
  91.5 0.1 select_bitcast_fusion
  91.6 0.0 copy-start.4
  91.7 0.1 reshape_squeeze.6
  91.8 0.1 reshape_squeeze.7
  91.8 0.4 fusion.41
  92.2 14.0 %all-gather = f32[32,4,4]{2,1,0:T(4,128)S(1)} all-gather(f32[4,4,4]{2,1,0:T(4,128)S(1)} %get-tuple-element.231), channel_id=2, replica_groups=mesh['groups'=2,'seq'=4,'head'=2,'rep'=2] {'seq','rep'}, dimensions={0}, use_global_device_ids=true | all-gather | bytes 2304 | tf_op jit(solution)/shard_map/all_gather | solution.py:21
  106.2 0.2 fusion.15
  106.4 0.2 fusion.5
  106.6 14.2 %all-gather.2 = f32[32,4,4,128]{3,2,1,0:T(4,128)S(1)} all-gather(f32[4,4,4,128]{3,2,1,0:T(4,128)S(1)} %fusion.5), channel_id=4, replica_groups=mesh['groups'=2,'seq'=4,'head'=2,'rep'=2] {'seq','rep'}, dimensions={0}, use_global_device_ids=true | all-gather | bytes 294912 | tf_op jit(solution)/shard_map/all_gather | solution.py:21
  120.9 14.0 %all-gather.1 = f32[32,4,4]{2,1,0:T(4,128)S(1)} all-gather(f32[4,4,4]{2,1,0:T(4,128)S(1)} %fusion.15), channel_id=3, replica_groups=mesh['groups'=2,'seq'=4,'head'=2,'rep'=2] {'seq','rep'}, dimensions={0}, use_global_device_ids=true | all-gather | bytes 2304 | tf_op jit(solution)/shard_map/all_gather | solution.py:21
  134.8 1.4 while.19
  134.9 0.1 fusion.56
  135.1 0.1 fusion.56
  135.3 0.1 fusion.56
  135.5 0.1 fusion.56
  135.7 0.1 fusion.56
  135.9 0.1 fusion.56
  136.1 0.1 fusion.56
  136.2 0.1 fusion.10
  136.4 2.0 fusion.44
  138.3 5.0 %psum.67 = f32[4,512]{1,0:T(4,128)S(1)} all-reduce(f32[4,512]{1,0:T(4,128)S(1)} %fusion.44), channel_id=1, replica_groups=mesh['groups'=2,'seq'=4,'head'=2,'rep'=2] {'head'}, use_global_device_ids=true, to_apply=%region_13.14 | all-reduce | flops 2048 | bytes 16384 | tf_op jit(solution)/shard_map/psum | solution.py:184
  143.3 0.1 multiply_reduce_fusion.1
  143.4 13.6 %psum.68 = f32[4]{0:T(128)S(1)} all-reduce(f32[4]{0:T(128)S(1)} %multiply_reduce_fusion.1), channel_id=1, replica_groups=mesh['groups'=2,'seq'=4,'head'=2,'rep'=2] {'seq','rep'}, use_global_device_ids=true, to_apply=%region_15.16 | all-reduce | flops 4 | bytes 32 | tf_op jit(solution)/shard_map/psum | solution.py:186
  157.0 3.4 %fusion.43 = f32[4,3584]{1,0:T(4,128)} fusion(bf16[512,3584]{1,0:T(8,128)(2,1)} %param.23, f32[512]{0:T(512)S(1)} %copy-done.4, f32[4]{0:T(128)S(1)} %add_rsqrt_fusion, f32[4,512]{1,0:T(4,128)S(1)} %psum.67, bf16[4,512]{1,0:T(4,128)(2,1)S(1)} %copy-done.2), kind=kOutput, calls=%fused_computation.89 | convolution fusion | flops 14690304 | bytes 3741712 | tf_op jit(solution)/shard_map/dot_general | solution.py:192
  160.5 1.2 fusion.42
  161.7 0.0 all-reduce.4.cloned.1.call-update
  161.7 0.8 copy.43
  162.6 50.4 %all-reduce.4.cloned.1.call-done = (f32[4,3584]{1,0:T(4,128)}, f32[4,3584]{1,0:T(4,128)}) async-done(((f32[4,3584]{1,0:T(4,128)}, f32[4,3584]{1,0:T(4,128)}), (f32[4,3584]{1,0:T(4,128)}, f32[4,3584]{1,0:T(4,128)})) %all-reduce.4.cloned.1.call-update) | async-done | bytes 114704 | tf_op jit(solution)/shard_map/psum | solution.py:190
  213.0 2.7 %fusion.11 = f32[4,512]{1,0:T(4,128)S(1)} fusion(bf16[3584,512]{1,0:T(8,128)(2,1)} %param.25, f32[4,3584]{1,0:T(4,128)} %get-tuple-element.207, f32[4,3584]{1,0:T(4,128)} %get-tuple-element.208), kind=kOutput, calls=%fused_computation.31 | convolution fusion | flops 14766080 | bytes 3792896 | tf_op jit(solution)/shard_map/dot_general | solution.py:198
  215.7 5.0 %psum.71 = f32[4,512]{1,0:T(4,128)S(1)} all-reduce(f32[4,512]{1,0:T(4,128)S(1)} %fusion.11), channel_id=1, replica_groups=mesh['groups'=2,'seq'=4,'head'=2,'rep'=2] {'head'}, use_global_device_ids=true, to_apply=%region_18.19 | all-reduce | flops 2048 | bytes 16384 | tf_op jit(solution)/shard_map/psum | solution.py:198
  220.7 0.6 add_convert_fusion.1
  (36 shorter events, 0.4 us)
Async XLA Ops:
  7.2 52.2 %copy-start = (bf16[512,2048]{1,0:T(8,128)(2,1)S(1)}, bf16[512,2048]{1,0:T(8,128)(2,1)}, u32[]{:S(2)}) copy-start(bf16[512,2048]{1,0:T(8,128)(2,1)} %param.19) | copy-start | bytes 6291460
  18.7 9.7 %copy-start.6 = (s32[4]{0:T(128)S(1)}, s32[4]{0:T(128)}, u32[]{:S(2)}) copy-start(s32[4]{0:T(128)} %param.27) | copy-start | bytes 52
  18.8 9.7 %copy-start.2 = (bf16[4,512]{1,0:T(4,128)(2,1)S(1)}, bf16[4,512]{1,0:T(4,128)(2,1)}, u32[]{:S(2)}) copy-start(bf16[4,512]{1,0:T(4,128)(2,1)} %param.16) | copy-start | bytes 12292
  18.8 38.1 %copy-start.3 = (f32[512]{0:T(512)S(1)}, f32[512]{0:T(512)}, u32[]{:S(2)}) copy-start(f32[512]{0:T(512)} %param.17) | copy-start | bytes 6148
  19.9 68.8 %copy-start.5 = (s32[4]{0:T(128)S(1)}, s32[4]{0:T(128)}, u32[]{:S(2)}) copy-start(s32[4]{0:T(128)} %param.28) | copy-start | bytes 52
  21.1 67.7 %all-to-all-start = ((bf16[2,1,8,64,512]{4,3,0,1,2:T(8,128)(2,1)}), bf16[2,1,8,64,512]{4,3,0,1,2:T(8,128)(2,1)S(1)}, u32[]{:S(2)}, u32[]{:S(2)}) async-start(bf16[2,1,8,64,512]{4,3,0,1,2:T(8,128)(2,1)} %bitcast.69), calls=%async_computation | async-start | bytes 2097152 | tf_op jit(solution)/shard_map/all_to_all | solution.py:169
  28.4 184.7 %all-reduce.4.cloned.1.call-start = ((), (), s32[]{:S(2)}) async-start(), calls=%async_computation.1 | async-start | bytes 229376 | tf_op jit(solution)/shard_map/psum | solution.py:190
  91.6 65.4 %copy-start.4 = (f32[512]{0:T(512)S(1)}, f32[512]{0:T(512)}, u32[]{:S(2)}) copy-start(f32[512]{0:T(512)} %param.18) | copy-start | bytes 6148
  157.0 3.4 %copy-start.1 = (bf16[512,3584]{1,0:T(8,128)(2,1)S(1)}, bf16[512,3584]{1,0:T(8,128)(2,1)}, u32[]{:S(2)}) copy-start(bf16[512,3584]{1,0:T(8,128)(2,1)} %param.24) | copy-start | bytes 11010052
Sparse Core Ops, SparseCore 0:
  161.9 51.1 all-reduce.3
where the time goes:
time: 229 us; the launch traced here: 228 us
  blocking collectives  122 us (53%)
  waiting for transfers between devices  50.5 us (22%)
  between operations  16.2 us (7%)
  matrix products  12.9 us (6%)
  other arithmetic  10.2 us (4%)
  local copies, waits for them, and re-layouts  8.65 us (4%)
  starting transfers between devices  7.32 us (3%)
    psum x1, waiting for transfers between devices, shards(): lax.psum((jnp.dot(normed_mid, w_gate, preferred_element_type=jnp.float32)...  50.4 us
    all_gather x3, blocking collectives, combined_all(): everything = jax.tree.map(lambda part: lax.all_gather(part, axis), value)  42.2 us
    psum x1, blocking collectives, shards(): square_sum = lax.psum(jnp.sum(residual * residual, axis=1), ('seq', 'rep'))  28.3 us
    psum x1, blocking collectives, shards(): lax.psum((jnp.dot(normed, w_query, preferred_element_type=jnp.float32), j...  28.2 us
    psum x1, blocking collectives, shards(): square_mid = lax.psum(jnp.sum(middle * middle, axis=1), ('seq', 'rep'))  13.6 us
    all_to_all x1, starting transfers between devices, shards(): lax.all_to_all(parted, ('seq', 'head'), split_axis=2, concat_axis=1, tile...  7.28 us
    psum x1, blocking collectives, shards(): lax.psum(jnp.dot(attn_heads, w_out, preferred_element_type=jnp.float32),...  4.97 us
    psum x1, blocking collectives, shards(): lax.psum(jnp.dot(hidden, w_down, preferred_element_type=jnp.float32), 'he...  4.97 us
  transfers between devices with their start and end apart: 2, of which 1 were waited for; matrix products, arithmetic and copies ran while one was open for 2% of the time, Pallas kernels for 0%

commit v1 on v0

v1 whole, which is shorter than its diff:
```python
import functools
import math

import jax
import jax.numpy as jnp
from jax import lax
from jax.experimental import pallas as pl
from jax.experimental.pallas import tpu as pltpu
from jax.sharding import PartitionSpec as P

HD = 128
EPSILON = 1e-05
ROPE_LOG = math.log(500000.0)
FLOOR_SCORE = -1e30
MESH = pl.DeviceIdType.MESH
F32 = jnp.float32
BF16 = jnp.bfloat16


def trig_rows(lengths):
    half_dim = HD // 2
    freq_table = jnp.exp(jnp.arange(half_dim, dtype=F32) * (-2.0 * ROPE_LOG / HD))
    angles = lengths.astype(F32)[:, None] * freq_table
    cosine = jnp.cos(angles)
    sine_part = jnp.sin(angles)
    return jnp.concatenate([cosine, cosine, -sine_part, sine_part], axis=-1)


def layer_kernel(
    dims,
    lengths_ref,
    row_ref,
    table_ref,
    trig_ref,
    tokens_ref,
    gain_ref,
    ffn_gain_ref,
    wq_hbm,
    wk_hbm,
    wv_hbm,
    wo_hbm,
    wg_hbm,
    wu_hbm,
    wd_hbm,
    pool_hbm,
    out_ref,
    kv_ref,
    wq,
    wk,
    wv,
    wo,
    wg,
    wu,
    wd,
    kvx,
    kvs,
    arr,
    tok,
    xp,
    qkv_part,
    qkv_recv,
    heads_buf,
    soft_part,
    soft_recv,
    attn_part,
    attn_recv,
    attn_rows,
    proj_part,
    proj_recv,
    mid_part,
    mid_recv,
    hid_part,
    hid_recv,
    hid_rows,
    down_part,
    down_recv,
    final,
    local_sem,
    kvx_send,
    kvx_recv,
    kvz_send,
    kvz_recv,
    qkv_send,
    qkv_rsem,
    soft_send,
    soft_rsem,
    attn_send,
    attn_rsem,
    proj_send,
    proj_rsem,
    mid_send,
    mid_rsem,
    hid_send,
    hid_rsem,
    down_send,
    down_rsem,
):
    n_seq, n_head, n_rep, width, block = dims
    seq_count = tokens_ref.shape[0]
    group = lax.axis_index("groups")
    s_me = lax.axis_index("seq")
    h_me = lax.axis_index("head")
    r_me = lax.axis_index("rep")
    n_ring = n_seq * n_rep
    me = s_me * n_rep + r_me

    def at_ring(peer):
        return (group, peer // n_rep, h_me, peer % n_rep)

    def at_head(peer):
        return (group, s_me, peer, r_me)

    def at_seq(peer):
        return (group, peer, h_me, r_me)

    def at_rep(peer):
        return (group, s_me, h_me, peer)

    def send_all(source_of, dst, count, mine, place, send, recv):
        copies = []
        for k in range(1, count):
            peer = lax.rem(mine + k, count)
            copy = pltpu.make_async_remote_copy(
                src_ref=source_of(peer),
                dst_ref=dst.at[mine],
                send_sem=send.at[k],
                recv_sem=recv.at[k],
                device_id=place(peer),
                device_id_type=MESH,
            )
            copy.start()
            copies.append(copy)
        return copies

    def arrive(copies):
        for copy in copies:
            copy.wait()

    half_feat = pool_hbm.shape[4] // n_head
    weights = []
    for j, (src, dst) in enumerate(
        ((wq_hbm, wq), (wk_hbm, wk), (wv_hbm, wv), (wo_hbm, wo), (wg_hbm, wg), (wu_hbm, wu), (wd_hbm, wd))
    ):
        copy = pltpu.make_async_copy(src, dst, local_sem.at[j])
        copy.start()
        weights.append(copy)

    def features_for(peer):
        return pool_hbm.at[:, 0, :, :, pl.ds(pl.multiple_of(peer * half_feat, HD), half_feat)]

    own_kv = pltpu.make_async_copy(features_for(h_me), kvx.at[h_me], local_sem.at[7])
    own_kv.start()

    barrier = pltpu.get_barrier_semaphore()
    for k in range(1, n_ring):
        pl.semaphore_signal(
            barrier, inc=1, device_id=at_ring(lax.rem(me + k, n_ring)), device_id_type=MESH
        )
    for k in range(1, n_head):
        pl.semaphore_signal(
            barrier, inc=1, device_id=at_head(lax.rem(h_me + k, n_head)), device_id_type=MESH
        )
    pl.semaphore_wait(barrier, n_ring + n_head - 2)

    kvx_copies = send_all(features_for, kvx, n_head, h_me, at_head, kvx_send, kvx_recv)

    tok[...] = tokens_ref[...].astype(F32)
    owner_here = jnp.int32(0)
    for p in range(seq_count):
        owner = jnp.int32(0)
        for i in range(seq_count):
            owner = jnp.where(row_ref[i] == p, i, owner)
        owner_here = jnp.where(s_me == p, owner, owner_here)
        xp[p : p + 1, :] = tok[pl.ds(owner, 1), :]
    length_here = lengths_ref[owner_here]

    residual = xp[...]
    squares = jnp.sum(residual * residual, axis=1, keepdims=True)
    scaled = (residual * gain_ref[...]).astype(BF16)
    q_cols, kv_cols = wq.shape[1], wk.shape[1]
    for copy in weights[:3]:
        copy.wait()
    q_part = jnp.dot(scaled, wq[...], preferred_element_type=F32)
    k_part = jnp.dot(scaled, wk[...], preferred_element_type=F32)
    v_part = jnp.dot(scaled, wv[...], preferred_element_type=F32)
    total = q_cols + 2 * kv_cols
    for s in range(seq_count):
        qkv_part[s, :, 0:q_cols] = q_part[s : s + 1]
        qkv_part[s, :, q_cols : q_cols + kv_cols] = k_part[s : s + 1]
        qkv_part[s, :, q_cols + kv_cols : total] = v_part[s : s + 1]
        qkv_part[s, :, total : total + HD] = jnp.broadcast_to(squares[s : s + 1], (1, HD))
    qkv_copies = send_all(
        lambda peer: qkv_part.at[peer // n_rep], qkv_recv, n_ring, me, at_ring, qkv_send, qkv_rsem
    )
    qkv_recv[me] = qkv_part[s_me]

    own_kv.wait()
    arrive(kvx_copies)
    slots_local = kvx.shape[2]
    half_rows = kvx.shape[3]
    blocks = table_ref.shape[1]
    for b in range(blocks):
        slot = table_ref[owner_here, b]
        holder = slot // slots_local
        local = lax.rem(slot, slots_local)
        first = b * block + r_me * half_rows
        live = lax.broadcasted_iota(jnp.int32, (half_rows, half_feat), 0) + first < length_here
        for c in range(2):
            rows = kvx[holder, c, local].astype(F32)
            kvs[b, c] = jnp.where(live, rows, 0.0).astype(BF16)

    arrive(qkv_copies)
    summed = jnp.sum(qkv_recv[...], axis=0)
    scale = lax.rsqrt(summed[:, total : total + HD] / width + EPSILON)
    heads = q_cols // HD
    kv_heads = kv_cols // HD
    for h in range(heads + 2 * kv_heads):
        heads_buf[h : h + 1, :] = summed[:, h * HD : (h + 1) * HD] * scale
    trig = trig_ref[pl.ds(owner_here, 1), :]
    queries = heads_buf[0:heads]
    keys_new = heads_buf[heads : heads + kv_heads]
    values_new = heads_buf[heads + kv_heads : heads + 2 * kv_heads].astype(BF16).astype(F32)

    def rotated(values):
        return (values * trig[:, :HD] + pltpu.roll(values, HD // 2, 1) * trig[:, HD:]).astype(BF16)

    rot_queries = rotated(queries)
    rot_keys = rotated(keys_new).astype(F32)
    factor = 1.0 / math.sqrt(HD)
    per_group = heads // kv_heads
    tokens_here = blocks * half_rows
    spot = lax.broadcasted_iota(jnp.int32, (per_group, tokens_here), 1)
    position = (spot // half_rows) * block + lax.rem(spot, half_rows) + r_me * half_rows
    usable = position < length_here
    for g in range(kv_heads):
        cols = slice(g * HD, (g + 1) * HD)
        mine = slice(g * per_group, (g + 1) * per_group)
        keys = kvs[:, 0, :, cols].reshape(tokens_here, HD)
        values = kvs[:, 1, :, cols].reshape(tokens_here, HD)
        scores = (
            lax.dot_general(
                rot_queries[mine], keys, (((1,), (1,)), ((), ())), preferred_element_type=F32
            )
            * factor
        )
        scores = jnp.where(usable, scores, FLOOR_SCORE)
        highest = jnp.max(scores, axis=1, keepdims=True)
        shares = jnp.where(usable, jnp.exp(scores - highest), 0.0)
        mass = jnp.sum(shares, axis=1, keepdims=True)
        soft_part[0, mine, :] = jnp.dot(shares.astype(BF16), values, preferred_element_type=F32)
        soft_part[1, mine, :] = jnp.broadcast_to(highest, (per_group, HD))
        soft_part[2, mine, :] = jnp.broadcast_to(mass, (per_group, HD))
    soft_copies = send_all(
        lambda peer: soft_part, soft_recv, n_rep, r_me, at_rep, soft_send, soft_rsem
    )
    soft_recv[r_me] = soft_part[...]
    own_key = jnp.concatenate(
        [jnp.broadcast_to(rot_keys[g : g + 1], (per_group, HD)) for g in range(kv_heads)], axis=0
    )
    own_value = jnp.concatenate(
        [jnp.broadcast_to(values_new[g : g + 1], (per_group, HD)) for g in range(kv_heads)], axis=0
    )
    own_score = jnp.sum(rot_queries.astype(F32) * own_key, axis=1, keepdims=True) * factor
    arrive(soft_copies)
    largest = jnp.broadcast_to(own_score, (heads, HD))
    for r in range(n_rep):
        largest = jnp.maximum(largest, soft_recv[r, 1])
    own_share = jnp.exp(own_score - largest)
    denominator = own_share
    mixed = own_share * own_value
    for r in range(n_rep):
        weight = jnp.exp(soft_recv[r, 1] - largest)
        denominator = denominator + soft_recv[r, 2] * weight
        mixed = mixed + soft_recv[r, 0] * weight
    attn_part[...] = (mixed / denominator).astype(BF16).astype(F32)
    attn_copies = send_all(
        lambda peer: attn_part, attn_recv, n_seq, s_me, at_seq, attn_send, attn_rsem
    )
    attn_recv[s_me] = attn_part[...]
    kvz_copies = send_all(lambda peer: kvs.at[peer], arr, n_seq, s_me, at_seq, kvz_send, kvz_recv)
    arr[s_me] = kvs[s_me]
    weights[3].wait()
    arrive(attn_copies)
    for s in range(seq_count):
        for h in range(heads):
            attn_rows[s : s + 1, h * HD : (h + 1) * HD] = attn_recv[s, h : h + 1, :]
    proj_part[...] = jnp.dot(attn_rows[...].astype(BF16), wo[...], preferred_element_type=F32)
    proj_copies = send_all(
        lambda peer: proj_part, proj_recv, n_head, h_me, at_head, proj_send, proj_rsem
    )
    proj_recv[h_me] = proj_part[...]
    for copy in weights[4:6]:
        copy.wait()
    arrive(proj_copies)
    middle = xp[...] + jnp.sum(proj_recv[...], axis=0)
    mid_squares = jnp.sum(middle * middle, axis=1, keepdims=True)
    mid_scaled = (middle * ffn_gain_ref[...]).astype(BF16)
    piece = wg.shape[1] // n_rep
    for j, weight in enumerate((wg, wu)):
        partial = jnp.dot(mid_scaled, weight[...], preferred_element_type=F32)
        for s in range(seq_count):
            for r in range(n_rep):
                mid_part[s * n_rep + r, :, j * piece : (j + 1) * piece] = partial[
                    s : s + 1, r * piece : (r + 1) * piece
                ]
    for s in range(seq_count):
        for r in range(n_rep):
            mid_part[s * n_rep + r, :, 2 * piece : 2 * piece + HD] = jnp.broadcast_to(
                mid_squares[s : s + 1], (1, HD)
            )
    mid_copies = send_all(
        lambda peer: mid_part.at[peer], mid_recv, n_ring, me, at_ring, mid_send, mid_rsem
    )
    mid_recv[me] = mid_part[me]
    arrive(mid_copies)
    sums = jnp.sum(mid_recv[...], axis=0)
    mid_scale = lax.rsqrt(sums[:, 2 * piece : 2 * piece + 1] / width + EPSILON)
    gate = sums[:, :piece] * mid_scale
    up = sums[:, piece : 2 * piece] * mid_scale
    hid_part[...] = (gate / (1.0 + jnp.exp(-gate)) * up).astype(BF16).astype(F32)
    hid_copies = send_all(
        lambda peer: hid_part, hid_recv, n_ring, me, at_ring, hid_send, hid_rsem
    )
    hid_recv[me] = hid_part[...]
    weights[6].wait()
    arrive(hid_copies)
    for s in range(seq_count):
        for r in range(n_rep):
            hid_rows[s : s + 1, r * piece : (r + 1) * piece] = hid_recv[s * n_rep + r]
    down_part[...] = jnp.dot(hid_rows[...].astype(BF16), wd[...], preferred_element_type=F32)
    down_copies = send_all(
        lambda peer: down_part, down_recv, n_head, h_me, at_head, down_send, down_rsem
    )
    down_recv[h_me] = down_part[...]
    arrive(kvz_copies)
    for i in range(seq_count):
        source = row_ref[i]
        for c in range(2):
            kv_ref[c, i] = arr[source, c]
    arrive(down_copies)
    final[...] = middle + jnp.sum(down_recv[...], axis=0)
    for i in range(seq_count):
        tok[i : i + 1, :] = final[pl.ds(row_ref[i], 1), :]
    out_ref[...] = tok[...].astype(BF16)


def shards(
    n_groups,
    n_seq,
    n_head,
    n_rep,
    tokens,
    attn_gain,
    ffn_gain,
    w_query,
    w_key,
    w_value,
    w_out,
    w_gate,
    w_up,
    w_down,
    kv_pool,
    lengths,
    pool_row,
    block_table,
):
    seq_count, cols = tokens.shape
    n_ring = n_seq * n_rep
    width = cols * n_ring
    _, _, slots_local, half_rows, feat = kv_pool.shape
    half_feat = feat // n_head
    blocks = block_table.shape[1]
    q_cols, kv_cols = w_query.shape[1], w_key.shape[1]
    heads, kv_heads = q_cols // HD, kv_cols // HD
    qkv = q_cols + 2 * kv_cols + HD
    piece = w_gate.shape[1] // n_rep
    vmem = pltpu.VMEM
    dma = pltpu.SemaphoreType.DMA
    hbm = pl.BlockSpec(memory_space=pltpu.HBM)
    in_v = pl.BlockSpec(memory_space=pltpu.VMEM)
    in_s = pl.BlockSpec(memory_space=pltpu.SMEM)
    weights = (w_query, w_key, w_value, w_out, w_gate, w_up, w_down)
    out, kv = pl.pallas_call(
        functools.partial(layer_kernel, (n_seq, n_head, n_rep, width, half_rows * n_rep)),
        out_shape=(
            jax.ShapeDtypeStruct((seq_count, cols), BF16),
            jax.ShapeDtypeStruct((2, seq_count, half_rows, half_feat), BF16),
        ),
        in_specs=[in_s] * 3 + [in_v] * 4 + [hbm] * 8,
        out_specs=(in_v, in_v),
        scratch_shapes=[vmem(w.shape, BF16) for w in weights]
        + [
            vmem((n_head, 2, slots_local, half_rows, half_feat), BF16),
            vmem((blocks, 2, half_rows, half_feat), BF16),
            vmem((n_seq, 2, half_rows, half_feat), BF16),
            vmem((seq_count, cols), F32),
            vmem((seq_count, cols), F32),
            vmem((seq_count, 1, qkv), F32),
            vmem((n_ring, 1, qkv), F32),
            vmem((heads + 2 * kv_heads, HD), F32),
            vmem((3, heads, HD), F32),
            vmem((n_rep, 3, heads, HD), F32),
            vmem((heads, HD), F32),
            vmem((n_seq, heads, HD), F32),
            vmem((seq_count, q_cols), F32),
            vmem((seq_count, cols), F32),
            vmem((n_head, seq_count, cols), F32),
            vmem((n_ring, 1, 2 * piece + HD), F32),
            vmem((n_ring, 1, 2 * piece + HD), F32),
            vmem((1, piece), F32),
            vmem((n_ring, 1, piece), F32),
            vmem((seq_count, n_rep * piece), F32),
            vmem((seq_count, cols), F32),
            vmem((n_head, seq_count, cols), F32),
            vmem((seq_count, cols), F32),
            dma((8,)),
        ]
        + [dma((count,)) for count in (n_head, n_seq, n_ring, n_rep, n_seq, n_head, n_ring, n_ring, n_head) for _ in range(2)],
        compiler_params=pltpu.CompilerParams(
            collective_id=0, has_side_effects=True, vmem_limit_bytes=60 * 1024 * 1024
        ),
    )(
        lengths,
        pool_row,
        block_table,
        trig_rows(lengths),
        tokens,
        attn_gain[None, :],
        ffn_gain[None, :],
        *weights,
        kv_pool,
    )
    return out, kv


def solution(mesh):
    in_specs = (
        P("groups", ("seq", "rep")),
        P(("seq", "rep")),
        P(("seq", "rep")),
        P(("seq", "rep"), "head"),
        P(("seq", "rep"), "head"),
        P(("seq", "rep"), "head"),
        P("head", ("seq", "rep")),
        P(("seq", "rep"), "head"),
        P(("seq", "rep"), "head"),
        P("head", ("seq", "rep")),
        P(None, ("groups", "seq"), "head", "rep", None),
        P("groups"),
        P("groups"),
        P("groups", None),
    )
    out_specs = (P("groups", ("seq", "rep")), P(None, "groups", ("seq", "rep"), "head"))
    sizes = [mesh.shape[name] for name in ("groups", "seq", "head", "rep")]
    return jax.shard_map(
        functools.partial(shards, *sizes),
        mesh=mesh,
        in_specs=in_specs,
        out_specs=out_specs,
        check_vma=False,
    )
```

time: 229 us -> 46.5 us (0.20)
  blocking collectives: 122 us -> 0 us
  waiting for transfers between devices: 50.5 us -> 0 us
  Pallas kernels: 0 us -> 41 us
  between operations: 16.2 us -> 0.64 us
  matrix products: 12.9 us -> 0 us
  other arithmetic: 10.2 us -> 1.46 us
  starting transfers between devices: 7.32 us -> 0 us
  local copies, waits for them, and re-layouts: 8.65 us -> 3.15 us
    psum x5 -> x0, blocking collectives: 80 us -> none  [the longest x1 28.3 us: shards(): square_sum = lax.psum(jnp.sum(residual * residual, axis=1), ('seq', 'rep'))]
    psum x1 -> x0, waiting for transfers between devices: 50.4 us -> none  [shards(): lax.psum((jnp.dot(normed_mid, w_gate, preferred_element_type=jnp.float32)...]
    all_gather x3 -> x0, blocking collectives: 42.2 us -> none  [combined_all(): everything = jax.tree.map(lambda part: lax.all_gather(part, axis), value)]
    pallas_call x0 -> x1, Pallas kernels: none -> 41 us  [shards(): pl.pallas_call(functools.partial(layer_kernel, (n_seq, n_head, n_rep, wid...]
    dot_general x9 -> x0, matrix products: 12.9 us -> none  [the longest x1 3.43 us: shards(): jnp.dot(normed_mid, w_gate, preferred_element_type=jnp.float32)]
    all_to_all x1 -> x0, starting transfers between devices: 7.28 us -> none  [shards(): lax.all_to_all(parted, ('seq', 'head'), split_axis=2, concat_axis=1, tile...]
    gather x3 -> x0, local copies, waits for them, and re-layouts: 4.02 us -> none  [the longest x2 3.44 us: shards(): picked = jnp.take(cleaned, jnp.clip(local_slot, 0, slot_count - 1), axis=1)]
    select_n x4 -> x0, other arithmetic: 3.39 us -> none  [the longest x2 1.56 us: shards(): decoded = jnp.take(by_row, pool_row, axis=1)]
  transfers between devices with their start and end apart: 2 -> 0, of which waited for: 1 -> 0; matrix products, arithmetic and copies ran while one was open for 2% -> 0% of each run, Pallas kernels for 0% -> 0%
where the time goes in v1:
time: 46.5 us; the launch traced here: 46.3 us
  Pallas kernels  41 us (88%)
  local copies, waits for them, and re-layouts  3.15 us (7%)
  other arithmetic  1.46 us (3%)
  between operations  0.64 us (1%)
    pallas_call x1, Pallas kernels, shards(): pl.pallas_call(functools.partial(layer_kernel, (n_seq, n_head, n_rep, wid...  41 us
    unnamed x2, local copies, waits for them, and re-layouts  3.15 us

profile of v1, /device:TPU:0, one launch (start us, length us, event | category | flops | bytes accessed | tf_op | source)
XLA Modules:
  0.0 46.3 jit_solution(11949294093352988129)
XLA Ops:
  0.6 0.7 %convert_element_type.3 = f32[4]{0:T(128)S(1)} convert(s32[4]{0:T(128)} %lengths_ref.1) | non-fusion elementwise | flops 4 | bytes 32 | tf_op jit(solution)/shard_map/convert_element_type | solution.py:23
  1.3 0.1 multiply_cosine_fusion
  1.4 0.7 %pad_maximum_fusion.trig_ref = f32[4,256]{1,0:T(4,128)} fusion(f32[4,64]{1,0:T(4,128)S(1)} %get-tuple-element.4, f32[4,64]{1,0:T(4,128)S(1)} %get-tuple-element.3, f32[4,64]{1,0:T(4,128)S(1)} %get-tuple-element.2), kind=kLoop, calls=%fused_computation | loop fusion | flops 3072 | bytes 7168 | tf_op jit(solution)/shard_map/concatenate | solution.py:26
  2.1 41.0 %shard_map.149 = (bf16[4,512]{1,0:T(4,128)(2,1)}, bf16[2,4,64,512]{3,2,1,0:T(8,128)(2,1)}) custom-call(s32[4]{0:T(128)} %lengths_ref.1, s32[4]{0:T(128)} %row_ref.1, s32[4,4]{1,0:T(4,128)} %table_ref.1, f32[4,256]{1,0:T(4,128)} %pad_maximum_fusion.trig_ref, bf16[4,512]{1,0:T(4,128)(2,1)} %tokens_ref.1, f32[1,512]{1,0:T(1,128)} %bitcast.2, f32[1,512]{1,0:T(1,128)} %bitcast.3, ...), custom_call_target="tpu_custom_call" | custom-call | tf_op jit(solution)/shard_map/pallas_call | solution.py:383
  43.1 1.3 %copy.18 = bf16[4,512]{1,0:T(4,128)(2,1)} copy(bf16[4,512]{1,0:T(4,128)(2,1)} %get-tuple-element.7) | data formatting | bytes 8192
  44.4 1.9 %copy.19 = bf16[2,4,64,512]{3,2,1,0:T(8,128)(2,1)} copy(bf16[2,4,64,512]{3,2,1,0:T(8,128)(2,1)} %get-tuple-element.8) | data formatting | bytes 1048576
  (1 shorter events, 0.0 us)

commit v2 on v1

--- a/solution.py
+++ b/solution.py
@@ -17,13 +17,22 @@
 BF16 = jnp.bfloat16
 
 
-def trig_rows(lengths):
+def round_up(count, unit):
+    return -(-count // unit) * unit
+
+
+def trig_rows(length):
     half_dim = HD // 2
-    freq_table = jnp.exp(jnp.arange(half_dim, dtype=F32) * (-2.0 * ROPE_LOG / HD))
-    angles = lengths.astype(F32)[:, None] * freq_table
-    cosine = jnp.cos(angles)
+    lane = lax.broadcasted_iota(jnp.int32, (8, HD), 1)
+    index = jnp.where(lane < half_dim, lane, lane - half_dim).astype(F32)
+    angles = length.astype(F32) * jnp.exp(index * (-2.0 * ROPE_LOG / HD))
     sine_part = jnp.sin(angles)
-    return jnp.concatenate([cosine, cosine, -sine_part, sine_part], axis=-1)
+    return jnp.cos(angles)[0:1], jnp.where(lane < half_dim, -sine_part, sine_part)[0:1]
+
+
+def high_low(values):
+    high = values.astype(BF16).astype(F32)
+    return high, values - high
 
 
 def layer_kernel(
@@ -31,7 +40,6 @@
     lengths_ref,
     row_ref,
     table_ref,
-    trig_ref,
     tokens_ref,
     gain_ref,
     ffn_gain_ref,
@@ -43,8 +51,8 @@
     wu_hbm,
     wd_hbm,
     pool_hbm,
-    out_ref,
-    kv_ref,
+    final,
+    arr,
     wq,
     wk,
     wv,
@@ -54,12 +62,12 @@
     wd,
     kvx,
     kvs,
-    arr,
     tok,
     xp,
     qkv_part,
     qkv_recv,
-    heads_buf,
+    qkv_send_buf,
+    split_buf,
     soft_part,
     soft_recv,
     attn_part,
@@ -68,18 +76,20 @@
     proj_part,
     proj_recv,
     mid_part,
+    mid_send_buf,
     mid_recv,
     hid_part,
     hid_recv,
     hid_rows,
     down_part,
     down_recv,
-    final,
     local_sem,
     kvx_send,
     kvx_recv,
     kvz_send,
     kvz_recv,
+    kvz_send2,
+    kvz_recv2,
     qkv_send,
     qkv_rsem,
     soft_send,
@@ -164,6 +174,8 @@
 
     kvx_copies = send_all(features_for, kvx, n_head, h_me, at_head, kvx_send, kvx_recv)
 
+    qkv_part[...] = jnp.zeros_like(qkv_part)
+    mid_part[...] = jnp.zeros_like(mid_part)
     tok[...] = tokens_ref[...].astype(F32)
     owner_here = jnp.int32(0)
     for p in range(seq_count):
@@ -175,54 +187,72 @@
     length_here = lengths_ref[owner_here]
 
     residual = xp[...]
-    squares = jnp.sum(residual * residual, axis=1, keepdims=True)
-    scaled = (residual * gain_ref[...]).astype(BF16)
-    q_cols, kv_cols = wq.shape[1], wk.shape[1]
-    for copy in weights[:3]:
-        copy.wait()
-    q_part = jnp.dot(scaled, wq[...], preferred_element_type=F32)
-    k_part = jnp.dot(scaled, wk[...], preferred_element_type=F32)
-    v_part = jnp.dot(scaled, wv[...], preferred_element_type=F32)
-    total = q_cols + 2 * kv_cols
-    for s in range(seq_count):
-        qkv_part[s, :, 0:q_cols] = q_part[s : s + 1]
-        qkv_part[s, :, q_cols : q_cols + kv_cols] = k_part[s : s + 1]
-        qkv_part[s, :, q_cols + kv_cols : total] = v_part[s : s + 1]
-        qkv_part[s, :, total : total + HD] = jnp.broadcast_to(squares[s : s + 1], (1, HD))
+    square_parts = high_low(jnp.sum(residual * residual, axis=1, keepdims=True))
+    trig_cos, trig_sin = trig_rows(length_here)
+    heads = wq.shape[1] // HD
+    kv_heads = wk.shape[1] // HD
+
+    def projected(values):
+        high, low = high_low(values)
+        split_buf[0:seq_count, :] = high
+        split_buf[seq_count : 2 * seq_count, :] = low
+        return split_buf[...].astype(BF16)
+
+    def product(operand, weight):
+        both = jnp.dot(operand, weight[...], preferred_element_type=F32)
+        return both[0:seq_count] + both[seq_count : 2 * seq_count]
+
+    scaled = projected(residual * gain_ref[...])
+    at = 0
+    for j, weight in enumerate((wq, wk, wv)):
+        weights[j].wait()
+        partial = product(scaled, weight)
+        for t in range(weight.shape[1] // HD):
+            for s in range(seq_count):
+                qkv_part[s, at : at + 1, :] = partial[s : s + 1, t * HD : (t + 1) * HD]
+            at += 1
+    for part in square_parts:
+        for s in range(seq_count):
+            qkv_part[s, at : at + 1, :] = jnp.broadcast_to(part[s : s + 1], (1, HD))
+        at += 1
+    qkv_send_buf[...] = qkv_part[...].astype(BF16)
+    qkv_recv[me] = qkv_send_buf[s_me]
     qkv_copies = send_all(
-        lambda peer: qkv_part.at[peer // n_rep], qkv_recv, n_ring, me, at_ring, qkv_send, qkv_rsem
-    )
-    qkv_recv[me] = qkv_part[s_me]
+        lambda peer: qkv_send_buf.at[peer // n_rep], qkv_recv, n_ring, me, at_ring, qkv_send, qkv_rsem
+    )
 
     own_kv.wait()
     arrive(kvx_copies)
     slots_local = kvx.shape[2]
     half_rows = kvx.shape[3]
     blocks = table_ref.shape[1]
-    for b in range(blocks):
-        slot = table_ref[owner_here, b]
-        holder = slot // slots_local
-        local = lax.rem(slot, slots_local)
-        first = b * block + r_me * half_rows
-        live = lax.broadcasted_iota(jnp.int32, (half_rows, half_feat), 0) + first < length_here
-        for c in range(2):
+    for c in range(2):
+        for b in range(blocks):
+            slot = table_ref[owner_here, b]
+            holder = slot // slots_local
+            local = lax.rem(slot, slots_local)
+            first = b * block + r_me * half_rows
+            live = lax.broadcasted_iota(jnp.int32, (half_rows, half_feat), 0) + first < length_here
             rows = kvx[holder, c, local].astype(F32)
-            kvs[b, c] = jnp.where(live, rows, 0.0).astype(BF16)
+            kvs[c, b] = jnp.where(live, rows, 0.0).astype(BF16)
+        if c == 0:
+            key_copies = send_all(
+                lambda peer: kvs.at[0, peer], arr.at[0], n_seq, s_me, at_seq, kvz_send, kvz_recv
+            )
+    kept = pltpu.make_async_copy(kvs.at[:, s_me], arr.at[:, s_me], local_sem.at[8])
+    kept.start()
 
     arrive(qkv_copies)
-    summed = jnp.sum(qkv_recv[...], axis=0)
-    scale = lax.rsqrt(summed[:, total : total + HD] / width + EPSILON)
-    heads = q_cols // HD
-    kv_heads = kv_cols // HD
-    for h in range(heads + 2 * kv_heads):
-        heads_buf[h : h + 1, :] = summed[:, h * HD : (h + 1) * HD] * scale
-    trig = trig_ref[pl.ds(owner_here, 1), :]
-    queries = heads_buf[0:heads]
-    keys_new = heads_buf[heads : heads + kv_heads]
-    values_new = heads_buf[heads + kv_heads : heads + 2 * kv_heads].astype(BF16).astype(F32)
+    summed = jnp.sum(qkv_recv[...].astype(F32), axis=0)
+    total = heads + 2 * kv_heads
+    scale = lax.rsqrt((summed[total : total + 1] + summed[total + 1 : total + 2]) / width + EPSILON)
+    summed = summed * scale
+    queries = summed[0:heads]
+    keys_new = summed[heads : heads + kv_heads]
+    values_new = summed[heads + kv_heads : total].astype(BF16).astype(F32)
 
     def rotated(values):
-        return (values * trig[:, :HD] + pltpu.roll(values, HD // 2, 1) * trig[:, HD:]).astype(BF16)
+        return (values * trig_cos + pltpu.roll(values, HD // 2, 1) * trig_sin).astype(BF16)
 
     rot_queries = rotated(queries)
     rot_keys = rotated(keys_new).astype(F32)
@@ -235,8 +265,8 @@
     for g in range(kv_heads):
         cols = slice(g * HD, (g + 1) * HD)
         mine = slice(g * per_group, (g + 1) * per_group)
-        keys = kvs[:, 0, :, cols].reshape(tokens_here, HD)
-        values = kvs[:, 1, :, cols].reshape(tokens_here, HD)
+        keys = kvs[0, :, :, cols].reshape(tokens_here, HD)
+        values = kvs[1, :, :, cols].reshape(tokens_here, HD)
         scores = (
             lax.dot_general(
                 rot_queries[mine], keys, (((1,), (1,)), ((), ())), preferred_element_type=F32
@@ -272,18 +302,20 @@
         weight = jnp.exp(soft_recv[r, 1] - largest)
         denominator = denominator + soft_recv[r, 2] * weight
         mixed = mixed + soft_recv[r, 0] * weight
-    attn_part[...] = (mixed / denominator).astype(BF16).astype(F32)
+    attn_part[...] = (mixed / denominator).astype(BF16)
     attn_copies = send_all(
         lambda peer: attn_part, attn_recv, n_seq, s_me, at_seq, attn_send, attn_rsem
     )
     attn_recv[s_me] = attn_part[...]
-    kvz_copies = send_all(lambda peer: kvs.at[peer], arr, n_seq, s_me, at_seq, kvz_send, kvz_recv)
-    arr[s_me] = kvs[s_me]
+    value_copies = send_all(
+        lambda peer: kvs.at[1, peer], arr.at[1], n_seq, s_me, at_seq, kvz_send2, kvz_recv2
+    )
     weights[3].wait()
     arrive(attn_copies)
     for s in range(seq_count):
+        gathered = attn_recv[s].astype(F32)
         for h in range(heads):
-            attn_rows[s : s + 1, h * HD : (h + 1) * HD] = attn_recv[s, h : h + 1, :]
+            attn_rows[s : s + 1, h * HD : (h + 1) * HD] = gathered[h : h + 1, :]
     proj_part[...] = jnp.dot(attn_rows[...].astype(BF16), wo[...], preferred_element_type=F32)
     proj_copies = send_all(
         lambda peer: proj_part, proj_recv, n_head, h_me, at_head, proj_send, proj_rsem
@@ -293,31 +325,37 @@
         copy.wait()
     arrive(proj_copies)
     middle = xp[...] + jnp.sum(proj_recv[...], axis=0)
-    mid_squares = jnp.sum(middle * middle, axis=1, keepdims=True)
-    mid_scaled = (middle * ffn_gain_ref[...]).astype(BF16)
-    piece = wg.shape[1] // n_rep
-    for j, weight in enumerate((wg, wu)):
-        partial = jnp.dot(mid_scaled, weight[...], preferred_element_type=F32)
+    mid_parts = high_low(jnp.sum(middle * middle, axis=1, keepdims=True))
+    mid_scaled = projected(middle * ffn_gain_ref[...])
+    tiles = wg.shape[1] // (n_rep * HD)
+    up_at = round_up(tiles + 2, 16)
+    for weight, start in ((wg, 0), (wu, up_at)):
+        partial = product(mid_scaled, weight)
         for s in range(seq_count):
             for r in range(n_rep):
-                mid_part[s * n_rep + r, :, j * piece : (j + 1) * piece] = partial[
-                    s : s + 1, r * piece : (r + 1) * piece
-                ]
-    for s in range(seq_count):
-        for r in range(n_rep):
-            mid_part[s * n_rep + r, :, 2 * piece : 2 * piece + HD] = jnp.broadcast_to(
-                mid_squares[s : s + 1], (1, HD)
-            )
+                for t in range(tiles):
+                    col = (r * tiles + t) * HD
+                    mid_part[s * n_rep + r, start + t : start + t + 1, :] = partial[
+                        s : s + 1, col : col + HD
+                    ]
+    for j, part in enumerate(mid_parts):
+        for s in range(seq_count):
+            for r in range(n_rep):
+                mid_part[s * n_rep + r, tiles + j : tiles + j + 1, :] = jnp.broadcast_to(
+                    part[s : s + 1], (1, HD)
+                )
+    mid_send_buf[...] = mid_part[...].astype(BF16)
+    mid_recv[me] = mid_send_buf[me]
     mid_copies = send_all(
-        lambda peer: mid_part.at[peer], mid_recv, n_ring, me, at_ring, mid_send, mid_rsem
-    )
-    mid_recv[me] = mid_part[me]
+        lambda peer: mid_send_buf.at[peer], mid_recv, n_ring, me, at_ring, mid_send, mid_rsem
+    )
     arrive(mid_copies)
-    sums = jnp.sum(mid_recv[...], axis=0)
-    mid_scale = lax.rsqrt(sums[:, 2 * piece : 2 * piece + 1] / width + EPSILON)
-    gate = sums[:, :piece] * mid_scale
-    up = sums[:, piece : 2 * piece] * mid_scale
-    hid_part[...] = (gate / (1.0 + jnp.exp(-gate)) * up).astype(BF16).astype(F32)
+    sums = jnp.sum(mid_recv[...].astype(F32), axis=0)
+    mid_scale = lax.rsqrt((sums[tiles : tiles + 1] + sums[tiles + 1 : tiles + 2]) / width + EPSILON)
+    tall = round_up(tiles, 16)
+    gate = sums[0:tall] * mid_scale
+    up = sums[up_at : up_at + tall] * mid_scale
+    hid_part[...] = (gate / (1.0 + jnp.exp(-gate)) * up).astype(BF16)
     hid_copies = send_all(
         lambda peer: hid_part, hid_recv, n_ring, me, at_ring, hid_send, hid_rsem
     )
@@ -326,22 +364,39 @@
     arrive(hid_copies)
     for s in range(seq_count):
         for r in range(n_rep):
-            hid_rows[s : s + 1, r * piece : (r + 1) * piece] = hid_recv[s * n_rep + r]
+            gathered = hid_recv[s * n_rep + r].astype(F32)
+            for t in range(tiles):
+                col = (r * tiles + t) * HD
+                hid_rows[s : s + 1, col : col + HD] = gathered[t : t + 1, :]
     down_part[...] = jnp.dot(hid_rows[...].astype(BF16), wd[...], preferred_element_type=F32)
     down_copies = send_all(
         lambda peer: down_part, down_recv, n_head, h_me, at_head, down_send, down_rsem
     )
     down_recv[h_me] = down_part[...]
-    arrive(kvz_copies)
-    for i in range(seq_count):
-        source = row_ref[i]
-        for c in range(2):
-            kv_ref[c, i] = arr[source, c]
+    arrive(key_copies)
+    arrive(value_copies)
+    kept.wait()
     arrive(down_copies)
     final[...] = middle + jnp.sum(down_recv[...], axis=0)
+
+
+def order_kernel(row_ref, final, arr, out_ref, kv_ref, held, ordered, load_sem, store_sem):
+    seq_count = final.shape[0]
+    loads, stores = [], []
     for i in range(seq_count):
-        tok[i : i + 1, :] = final[pl.ds(row_ref[i], 1), :]
-    out_ref[...] = tok[...].astype(BF16)
+        copy = pltpu.make_async_copy(arr.at[:, row_ref[i]], held.at[:, i], load_sem.at[i])
+        copy.start()
+        loads.append(copy)
+    for i in range(seq_count):
+        ordered[i : i + 1, :] = final[pl.ds(row_ref[i], 1), :]
+    out_ref[...] = ordered[...].astype(BF16)
+    for i in range(seq_count):
+        loads[i].wait()
+        copy = pltpu.make_async_copy(held.at[:, i], kv_ref.at[:, i], store_sem.at[i])
+        copy.start()
+        stores.append(copy)
+    for copy in stores:
+        copy.wait()
 
 
 def shards(
@@ -372,50 +427,52 @@
     blocks = block_table.shape[1]
     q_cols, kv_cols = w_query.shape[1], w_key.shape[1]
     heads, kv_heads = q_cols // HD, kv_cols // HD
-    qkv = q_cols + 2 * kv_cols + HD
-    piece = w_gate.shape[1] // n_rep
+    qkv = round_up(heads + 2 * kv_heads + 2, 16)
+    tiles = w_gate.shape[1] // (n_rep * HD)
+    tall = round_up(tiles, 16)
+    mid = round_up(tiles + 2, 16) + tall
     vmem = pltpu.VMEM
     dma = pltpu.SemaphoreType.DMA
     hbm = pl.BlockSpec(memory_space=pltpu.HBM)
     in_v = pl.BlockSpec(memory_space=pltpu.VMEM)
     in_s = pl.BlockSpec(memory_space=pltpu.SMEM)
     weights = (w_query, w_key, w_value, w_out, w_gate, w_up, w_down)
-    out, kv = pl.pallas_call(
+    final, arr = pl.pallas_call(
         functools.partial(layer_kernel, (n_seq, n_head, n_rep, width, half_rows * n_rep)),
         out_shape=(
-            jax.ShapeDtypeStruct((seq_count, cols), BF16),
-            jax.ShapeDtypeStruct((2, seq_count, half_rows, half_feat), BF16),
+            jax.ShapeDtypeStruct((seq_count, cols), F32),
+            jax.ShapeDtypeStruct((2, n_seq, half_rows, half_feat), BF16),
         ),
-        in_specs=[in_s] * 3 + [in_v] * 4 + [hbm] * 8,
-        out_specs=(in_v, in_v),
+        in_specs=[in_s] * 3 + [in_v] * 3 + [hbm] * 8,
+        out_specs=(in_v, hbm),
         scratch_shapes=[vmem(w.shape, BF16) for w in weights]
         + [
             vmem((n_head, 2, slots_local, half_rows, half_feat), BF16),
-            vmem((blocks, 2, half_rows, half_feat), BF16),
-            vmem((n_seq, 2, half_rows, half_feat), BF16),
+            vmem((2, blocks, half_rows, half_feat), BF16),
             vmem((seq_count, cols), F32),
             vmem((seq_count, cols), F32),
-            vmem((seq_count, 1, qkv), F32),
-            vmem((n_ring, 1, qkv), F32),
-            vmem((heads + 2 * kv_heads, HD), F32),
+            vmem((seq_count, qkv, HD), F32),
+            vmem((n_ring, qkv, HD), BF16),
+            vmem((seq_count, qkv, HD), BF16),
+            vmem((2 * seq_count, cols), F32),
             vmem((3, heads, HD), F32),
             vmem((n_rep, 3, heads, HD), F32),
-            vmem((heads, HD), F32),
-            vmem((n_seq, heads, HD), F32),
+            vmem((heads, HD), BF16),
+            vmem((n_seq, heads, HD), BF16),
             vmem((seq_count, q_cols), F32),
             vmem((seq_count, cols), F32),
             vmem((n_head, seq_count, cols), F32),
-            vmem((n_ring, 1, 2 * piece + HD), F32),
-            vmem((n_ring, 1, 2 * piece + HD), F32),
-            vmem((1, piece), F32),
-            vmem((n_ring, 1, piece), F32),
-            vmem((seq_count, n_rep * piece), F32),
+            vmem((n_ring, mid, HD), F32),
+            vmem((n_ring, mid, HD), BF16),
+            vmem((n_ring, mid, HD), BF16),
+            vmem((tall, HD), BF16),
+            vmem((n_ring, tall, HD), BF16),
+            vmem((seq_count, w_gate.shape[1]), F32),
             vmem((seq_count, cols), F32),
             vmem((n_head, seq_count, cols), F32),
-            vmem((seq_count, cols), F32),
-            dma((8,)),
+            dma((9,)),
         ]
-        + [dma((count,)) for count in (n_head, n_seq, n_ring, n_rep, n_seq, n_head, n_ring, n_ring, n_head) for _ in range(2)],
+        + [dma((count,)) for count in (n_head, n_seq, n_seq, n_ring, n_rep, n_seq, n_head, n_ring, n_ring, n_head) for _ in range(2)],
         compiler_params=pltpu.CompilerParams(
             collective_id=0, has_side_effects=True, vmem_limit_bytes=60 * 1024 * 1024
         ),
@@ -423,14 +480,27 @@
         lengths,
         pool_row,
         block_table,
-        trig_rows(lengths),
         tokens,
         attn_gain[None, :],
         ffn_gain[None, :],
         *weights,
         kv_pool,
     )
-    return out, kv
+    return pl.pallas_call(
+        order_kernel,
+        out_shape=(
+            jax.ShapeDtypeStruct((seq_count, cols), BF16),
+            jax.ShapeDtypeStruct((2, seq_count, half_rows, half_feat), BF16),
+        ),
+        in_specs=[in_s, in_v, hbm],
+        out_specs=(in_v, hbm),
+        scratch_shapes=[
+            vmem((2, seq_count, half_rows, half_feat), BF16),
+            vmem((seq_count, cols), F32),
+            dma((seq_count,)),
+            dma((seq_count,)),
+        ],
+    )(pool_row, final, arr)
 
 
 def solution(mesh):

time: 46.5 us -> 44.3 us (0.953)
  local copies, waits for them, and re-layouts: 3.15 us -> 0 us
  Pallas kernels: 41 us -> 43.4 us
  other arithmetic: 1.46 us -> 0 us
    unnamed x2 -> x0, local copies, waits for them, and re-layouts: 3.15 us -> none
    pallas_call x0 -> x1, Pallas kernels: none -> 3.12 us  [shards(): pl.pallas_call(order_kernel, out_shape=(jax.ShapeDtypeStruct((seq_count,...]
    pallas_call x1, Pallas kernels: 41 us -> 40.3 us  [shards(): pl.pallas_call(functools.partial(layer_kernel, (n_seq, n_head, n_rep, wid...]
    concatenate x1 -> x0, other arithmetic: 0.67 us -> none  [trig_rows(): return jnp.concatenate([cosine, cosine, -sine_part, sine_part], axis=-1)]
    convert_element_type x1 -> x0, other arithmetic: 0.66 us -> none  [trig_rows(): angles = lengths.astype(F32)[:, None] * freq_table]
where the time goes in v2:
time: 44.3 us; the launch traced here: 44.1 us
  Pallas kernels  43.4 us (98%)
  between operations  0.64 us (1%)
    pallas_call x1, Pallas kernels, shards(): pl.pallas_call(functools.partial(layer_kernel, (n_seq, n_head, n_rep, wid...  40.3 us
    pallas_call x1, Pallas kernels, shards(): pl.pallas_call(order_kernel, out_shape=(jax.ShapeDtypeStruct((seq_count,...  3.12 us

profile of v2, /device:TPU:0, one launch (start us, length us, event | category | flops | bytes accessed | tf_op | source)
XLA Modules:
  0.0 44.1 jit_solution(4522994328263089912)
XLA Ops:
  0.6 40.3 %shard_map.149 = (f32[4,512]{1,0:T(4,128)}, bf16[2,4,64,512]{3,2,1,0:T(8,128)(2,1)}) custom-call(s32[4]{0:T(128)} %lengths_ref.1, s32[4]{0:T(128)} %row_ref.3, s32[4,4]{1,0:T(4,128)} %table_ref.1, bf16[4,512]{1,0:T(4,128)(2,1)} %tokens_ref.1, f32[1,512]{1,0:T(1,128)} %bitcast.2, f32[1,512]{1,0:T(1,128)} %bitcast.3, bf16[512,2048]{1,0:T(8,128)(2,1)} %wq_hbm.1, ...), custom_call_target="tpu_custom_call" | custom-call | tf_op jit(solution)/shard_map/pallas_call | solution.py:440
  40.9 3.1 %shard_map.150 = (bf16[4,512]{1,0:T(4,128)(2,1)}, bf16[2,4,64,512]{3,2,1,0:T(8,128)(2,1)}) custom-call(s32[4]{0:T(128)} %row_ref.3, f32[4,512]{1,0:T(4,128)} %get-tuple-element.4.final, bf16[2,4,64,512]{3,2,1,0:T(8,128)(2,1)} %get-tuple-element.5.arr), custom_call_target="tpu_custom_call" | custom-call | tf_op jit(solution)/shard_map/pallas_call | solution.py:489

commit v3 on v2

--- a/solution.py
+++ b/solution.py
@@ -90,6 +90,8 @@
     kvz_recv,
     kvz_send2,
     kvz_recv2,
+    kvz_send3,
+    kvz_recv3,
     qkv_send,
     qkv_rsem,
     soft_send,
@@ -152,7 +154,8 @@
         ((wq_hbm, wq), (wk_hbm, wk), (wv_hbm, wv), (wo_hbm, wo), (wg_hbm, wg), (wu_hbm, wu), (wd_hbm, wd))
     ):
         copy = pltpu.make_async_copy(src, dst, local_sem.at[j])
-        copy.start()
+        if j < 3:
+            copy.start()
         weights.append(copy)
 
     def features_for(peer):
@@ -215,6 +218,8 @@
         for s in range(seq_count):
             qkv_part[s, at : at + 1, :] = jnp.broadcast_to(part[s : s + 1], (1, HD))
         at += 1
+    for copy in weights[3:]:
+        copy.start()
     qkv_send_buf[...] = qkv_part[...].astype(BF16)
     qkv_recv[me] = qkv_send_buf[s_me]
     qkv_copies = send_all(
@@ -235,10 +240,6 @@
             live = lax.broadcasted_iota(jnp.int32, (half_rows, half_feat), 0) + first < length_here
             rows = kvx[holder, c, local].astype(F32)
             kvs[c, b] = jnp.where(live, rows, 0.0).astype(BF16)
-        if c == 0:
-            key_copies = send_all(
-                lambda peer: kvs.at[0, peer], arr.at[0], n_seq, s_me, at_seq, kvz_send, kvz_recv
-            )
     kept = pltpu.make_async_copy(kvs.at[:, s_me], arr.at[:, s_me], local_sem.at[8])
     kept.start()
 
@@ -307,8 +308,18 @@
         lambda peer: attn_part, attn_recv, n_seq, s_me, at_seq, attn_send, attn_rsem
     )
     attn_recv[s_me] = attn_part[...]
-    value_copies = send_all(
-        lambda peer: kvs.at[1, peer], arr.at[1], n_seq, s_me, at_seq, kvz_send2, kvz_recv2
+    part_rows = half_rows // 2
+    early_copies = send_all(
+        lambda peer: kvs.at[0, peer], arr.at[0], n_seq, s_me, at_seq, kvz_send, kvz_recv
+    )
+    early_copies += send_all(
+        lambda peer: kvs.at[1, peer, pl.ds(0, part_rows)],
+        arr.at[1, :, pl.ds(0, part_rows)],
+        n_seq,
+        s_me,
+        at_seq,
+        kvz_send2,
+        kvz_recv2,
     )
     weights[3].wait()
     arrive(attn_copies)
@@ -349,6 +360,15 @@
     mid_copies = send_all(
         lambda peer: mid_send_buf.at[peer], mid_recv, n_ring, me, at_ring, mid_send, mid_rsem
     )
+    late_copies = send_all(
+        lambda peer: kvs.at[1, peer, pl.ds(part_rows, part_rows)],
+        arr.at[1, :, pl.ds(part_rows, part_rows)],
+        n_seq,
+        s_me,
+        at_seq,
+        kvz_send3,
+        kvz_recv3,
+    )
     arrive(mid_copies)
     sums = jnp.sum(mid_recv[...].astype(F32), axis=0)
     mid_scale = lax.rsqrt((sums[tiles : tiles + 1] + sums[tiles + 1 : tiles + 2]) / width + EPSILON)
@@ -373,28 +393,23 @@
         lambda peer: down_part, down_recv, n_head, h_me, at_head, down_send, down_rsem
     )
     down_recv[h_me] = down_part[...]
-    arrive(key_copies)
-    arrive(value_copies)
+    arrive(early_copies)
+    arrive(late_copies)
     kept.wait()
     arrive(down_copies)
     final[...] = middle + jnp.sum(down_recv[...], axis=0)
 
 
-def order_kernel(row_ref, final, arr, out_ref, kv_ref, held, ordered, load_sem, store_sem):
+def order_kernel(row_ref, final, arr, out_ref, kv_ref, ordered, store_sem):
     seq_count = final.shape[0]
-    loads, stores = [], []
+    stores = []
     for i in range(seq_count):
-        copy = pltpu.make_async_copy(arr.at[:, row_ref[i]], held.at[:, i], load_sem.at[i])
+        copy = pltpu.make_async_copy(arr.at[:, row_ref[i]], kv_ref.at[:, i], store_sem.at[i])
         copy.start()
-        loads.append(copy)
+        stores.append(copy)
     for i in range(seq_count):
         ordered[i : i + 1, :] = final[pl.ds(row_ref[i], 1), :]
     out_ref[...] = ordered[...].astype(BF16)
-    for i in range(seq_count):
-        loads[i].wait()
-        copy = pltpu.make_async_copy(held.at[:, i], kv_ref.at[:, i], store_sem.at[i])
-        copy.start()
-        stores.append(copy)
     for copy in stores:
         copy.wait()
 
@@ -472,7 +487,7 @@
             vmem((n_head, seq_count, cols), F32),
             dma((9,)),
         ]
-        + [dma((count,)) for count in (n_head, n_seq, n_seq, n_ring, n_rep, n_seq, n_head, n_ring, n_ring, n_head) for _ in range(2)],
+        + [dma((count,)) for count in (n_head, n_seq, n_seq, n_seq, n_ring, n_rep, n_seq, n_head, n_ring, n_ring, n_head) for _ in range(2)],
         compiler_params=pltpu.CompilerParams(
             collective_id=0, has_side_effects=True, vmem_limit_bytes=60 * 1024 * 1024
         ),
@@ -492,12 +507,10 @@
             jax.ShapeDtypeStruct((seq_count, cols), BF16),
             jax.ShapeDtypeStruct((2, seq_count, half_rows, half_feat), BF16),
         ),
-        in_specs=[in_s, in_v, hbm],
+        in_specs=[in_s, in_v, in_v],
         out_specs=(in_v, hbm),
         scratch_shapes=[
-            vmem((2, seq_count, half_rows, half_feat), BF16),
             vmem((seq_count, cols), F32),
-            dma((seq_count,)),
             dma((seq_count,)),
         ],
     )(pool_row, final, arr)

time: 44.3 us -> 41.2 us (0.930)
  Pallas kernels: 43.4 us -> 40.4 us
    pallas_call x1, Pallas kernels: 40.3 us -> 37.9 us  [shards(): pl.pallas_call(functools.partial(layer_kernel, (n_seq, n_head, n_rep, wid...]
    pallas_call x1, Pallas kernels: 3.12 us -> 2.48 us  [shards(): pl.pallas_call(order_kernel, out_shape=(jax.ShapeDtypeStruct((seq_count,...]
where the time goes in v3:
time: 41.2 us; the launch traced here: 41 us
  Pallas kernels  40.4 us (98%)
  between operations  0.64 us (2%)
    pallas_call x1, Pallas kernels, shards(): pl.pallas_call(functools.partial(layer_kernel, (n_seq, n_head, n_rep, wid...  37.9 us
    pallas_call x1, Pallas kernels, shards(): pl.pallas_call(order_kernel, out_shape=(jax.ShapeDtypeStruct((seq_count,...  2.48 us

profile of v3, /device:TPU:0, one launch (start us, length us, event | category | flops | bytes accessed | tf_op | source)
XLA Modules:
  0.0 41.0 jit_solution(13874885587323877285)
XLA Ops:
  0.6 37.9 %shard_map.149 = (f32[4,512]{1,0:T(4,128)}, bf16[2,4,64,512]{3,2,1,0:T(8,128)(2,1)}) custom-call(s32[4]{0:T(128)} %lengths_ref.1, s32[4]{0:T(128)} %row_ref.3, s32[4,4]{1,0:T(4,128)} %table_ref.1, bf16[4,512]{1,0:T(4,128)(2,1)} %tokens_ref.1, f32[1,512]{1,0:T(1,128)} %bitcast.2, f32[1,512]{1,0:T(1,128)} %bitcast.3, bf16[512,2048]{1,0:T(8,128)(2,1)} %wq_hbm.1, ...), custom_call_target="tpu_custom_call" | custom-call | tf_op jit(solution)/shard_map/pallas_call | solution.py:455
  38.6 2.5 %shard_map.150 = (bf16[4,512]{1,0:T(4,128)(2,1)}, bf16[2,4,64,512]{3,2,1,0:T(8,128)(2,1)}) custom-call(s32[4]{0:T(128)} %row_ref.3, f32[4,512]{1,0:T(4,128)} %get-tuple-element.4.final, bf16[2,4,64,512]{3,2,1,0:T(8,128)(2,1)} %get-tuple-element.5.arr), custom_call_target="tpu_custom_call" | custom-call | tf_op jit(solution)/shard_map/pallas_call | solution.py:504
